TPU v7x, 16 devices: a 4x2x1 block of a 4x4x8 slice. The times are simulated.
16 devices in a mesh: rep: 2 (over y, z), dp: 8 (over x, core).
Axes of the slice: x: 4, y: 2, z: 1, core: 2. Of those that a mesh axis runs over, the one named last changes fastest.
The devices are a block of a 4x4x8 slice.
Arguments:
- x: bfloat16 [16, 1024, 512], P(('rep', 'dp')), parts along dimension 0
- dy: bfloat16 [16, 1024, 512], P(('rep', 'dp')), parts along dimension 0
- w_gate: bfloat16 [2, 512, 8192], replicated
- w_up: bfloat16 [2, 512, 8192], replicated
- w_down: bfloat16 [2, 8192, 512], replicated
- m_w_gate: float32 [2, 512, 8192], P(None, 'dp')
- m_w_up: float32 [2, 512, 8192], P(None, 'dp')
- m_w_down: float32 [2, 8192, 512], P(None, 'dp')
- v_w_gate: float32 [2, 512, 8192], P(None, 'dp')
- v_w_up: float32 [2, 512, 8192], P(None, 'dp')
- v_w_down: float32 [2, 8192, 512], P(None, 'dp')
Outputs:
- output 1: bfloat16 [4, 512, 8192], P('rep'), parts along dimension 0
- output 2: bfloat16 [4, 512, 8192], P('rep'), parts along dimension 0
- output 3: bfloat16 [4, 8192, 512], P('rep'), parts along dimension 0
- output 4: float32 [4, 512, 8192], P('rep', 'dp'), parts along dimension 0
- output 5: float32 [4, 512, 8192], P('rep', 'dp'), parts along dimension 0
- output 6: float32 [4, 8192, 512], P('rep', 'dp'), parts along dimension 0
- output 7: float32 [4, 512, 8192], P('rep', 'dp'), parts along dimension 0
- output 8: float32 [4, 512, 8192], P('rep', 'dp'), parts along dimension 0
- output 9: float32 [4, 8192, 512], P('rep', 'dp'), parts along dimension 0
There are 2 independent parts. A program takes and returns all parts, laid end to end along the dimension named above; an argument that names none is the same for every part.
All inputs are finite; a program needn't handle non-finite values.
Results may differ from a plain program's by a relative error of at most 0.022.
Values are sent between devices in bfloat16 or wider.
A program may use at most 768 MiB of HBM per device.

v0:
```python
import jax
import jax.numpy as jnp
from jax import lax

NAMES = ("w_gate", "w_up", "w_down")


def matmul(a, w):
    return jnp.dot(a, w, preferred_element_type=jnp.float32).astype(jnp.bfloat16)


def normed(h):
    wide = h.astype(jnp.float32)
    scale = lax.rsqrt(jnp.mean(wide**2, -1, keepdims=True) + 1e-6)
    return (wide * scale).astype(jnp.bfloat16)


def layer(h, w):
    a = normed(h)
    gate = jnp.dot(a, w["w_gate"], preferred_element_type=jnp.float32)
    up = jnp.dot(a, w["w_up"], preferred_element_type=jnp.float32)
    return h + matmul((jax.nn.silu(gate) * up).astype(jnp.bfloat16), w["w_down"])


def adamw(w, m, v, g):
    m = 0.9 * m + 0.1 * g
    v = 0.95 * v + 0.05 * g * g
    step = m * lax.rsqrt(v + 1e-8) + 0.1 * w
    return (w - 0.02 * step).astype(jnp.bfloat16), m, v


def clipped(gradients, sum_of_squares, count):
    factor = jnp.minimum(1.0, 0.5 * lax.rsqrt(sum_of_squares / count + 1e-30))
    return [g * factor for g in gradients]


def stack(weights, h):
    for number in range(weights["w_gate"].shape[0]):
        h = layer(h, {name: w[number] for name, w in weights.items()})
    return h


def solution(mesh):
    groups = mesh.shape["rep"]

    def step(x, dy, *arrays):
        weights, m, v = (arrays[i : i + 3] for i in (0, 3, 6))
        x, dy = (t.reshape(groups, -1, *t.shape[1:]) for t in (x, dy))

        def of_a_group(x, dy):
            _, back = jax.vjp(lambda w: stack(w, x), dict(zip(NAMES, weights, strict=True)))
            by_weights = back(dy)[0]
            gradients = [by_weights[name].astype(jnp.float32) for name in NAMES]
            gradients = clipped(gradients, sum(jnp.sum(g * g) for g in gradients), sum(g.size for g in gradients))
            new = [adamw(w.astype(jnp.float32), m, v, g) for w, m, v, g in zip(weights, m, v, gradients, strict=True)]
            return tuple(one[which] for which in range(3) for one in new)

        return tuple(t.reshape(-1, *t.shape[2:]) for t in jax.vmap(of_a_group)(x, dy))

    return step
```

profile of v0, /device:TPU:113, one launch (start us, length us, event | category | flops | bytes accessed | tf_op | source)
XLA Modules:
  0.0 1094.2 jit_solution(7891357414864250700)
XLA Ops:
  10.3 19.3 %fusion.60 = f32[1024,8192]{1,0:T(8,128)} fusion(bf16[2,512,8192]{2,1,0:T(8,128)(2,1)} %param, bf16[1,1024,512]{2,1,0:T(8,128)(2,1)} %param.2, f32[1024]{0:T(1024)S(1)} %add_rsqrt_fusion), kind=kOutput, calls=%fused_computation.64 | convolution fusion | flops 8591507456 | bytes 42995712 | tf_op jit(solution)/vmap(jvp())/dot_general | solution.py:20
  29.6 18.0 %fusion.58 = f32[1024,8192]{1,0:T(8,128)} fusion(bf16[2,512,8192]{2,1,0:T(8,128)(2,1)} %param.3, bf16[1,1024,512]{2,1,0:T(8,128)(2,1)S(1)} %copy-done.6, f32[1024]{0:T(1024)S(1)} %add_rsqrt_fusion), kind=kOutput, calls=%fused_computation.62 | convolution fusion | flops 8591507456 | bytes 42995712 | tf_op jit(solution)/vmap(jvp())/dot_general | solution.py:21
  47.6 27.4 %fusion.26 = bf16[1024,8192]{1,0:T(8,128)(2,1)} fusion(f32[1024,8192]{1,0:T(8,128)} %fusion.58, f32[1024,8192]{1,0:T(8,128)} %fusion.60), kind=kLoop, calls=%fused_computation.35 | loop fusion | flops 50331648 | bytes 83886080
  90.0 19.1 %fusion.47 = f32[1024,8192]{1,0:T(8,128)} fusion(bf16[2,512,8192]{2,1,0:T(8,128)(2,1)} %param, bf16[1,1,1024,512]{2,3,1,0:T(8,128)(2,1)S(1)} %get-tuple-element.10, f32[1024]{0:T(1024)S(1)} %bitcast.371), kind=kOutput, calls=%fused_computation.51 | convolution fusion | flops 8591507456 | bytes 42995712 | tf_op jit(solution)/vmap(jvp())/dot_general | solution.py:20
  109.2 18.8 %fusion.51 = f32[1024,8192]{1,0:T(8,128)} fusion(bf16[2,512,8192]{2,1,0:T(8,128)(2,1)} %param.3, bf16[1,1,1024,512]{2,3,1,0:T(8,128)(2,1)S(1)} %get-tuple-element.10, f32[1024]{0:T(1024)S(1)} %bitcast.372), kind=kOutput, calls=%fused_computation.55 | convolution fusion | flops 8591507456 | bytes 42995712 | tf_op jit(solution)/vmap(jvp())/dot_general | solution.py:21
  143.7 33.4 %fusion.6 = bf16[1024,8192]{1,0:T(8,128)(2,1)} fusion(f32[1024,8192]{1,0:T(8,128)} %fusion.47, f32[1024,8192]{1,0:T(8,128)} %fusion.51, bf16[1024,8192]{1,0:T(8,128)(2,1)} %convolution_convert_fusion.1), kind=kLoop, calls=%fused_computation.11 | loop fusion | flops 100663296 | bytes 100663296
  177.1 15.6 %fusion.114 = bf16[1024,512]{0,1:T(8,128)(2,1)} fusion(bf16[1024,8192]{1,0:T(8,128)(2,1)} %fusion.6, bf16[2,512,8192]{2,1,0:T(8,128)(2,1)} %param), kind=kOutput, calls=%fused_computation.142 | convolution fusion | flops 8589934592 | bytes 26214400 | tf_op jit(solution)/vmap(transpose(jvp()))/dot_general | solution.py:20
  192.7 24.3 %fusion.107 = (f32[1024]{0:T(1024)S(1)}, bf16[1,1,1024,512]{2,3,1,0:T(8,128)(2,1)}) fusion(bf16[1,1,1024,512]{2,3,1,0:T(8,128)(2,1)S(1)} %get-tuple-element.10, bf16[1024,512]{0,1:T(8,128)(2,1)} %fusion.114, bf16[2,512,8192]{2,1,0:T(8,128)(2,1)} %param.3, bf16[1024,8192]{1,0:T(8,128)(2,1)} %convolution_convert_fusion.1, f32[1024,8192]{1,0:T(8,128)} %fusion.47), kind=kOutput, calls=%fused_computation.133 | convolution fusion | flops 8643410944 | bytes 61870080 | tf_op jit(solution)/vmap(transpose(jvp()))/dot_general | solution.py:21
  220.0 16.0 %convolution_bitcast_fusion = f32[1,8192,512]{2,1,0:T(8,128)} fusion(bf16[1024,8192]{1,0:T(8,128)(2,1)} %fusion.26, bf16[1024,512]{0,1:T(8,128)(2,1)S(1)} %fusion.141), kind=kOutput, calls=%fused_computation.49 | convolution fusion | flops 8589934592 | bytes 34603008 | tf_op jit(solution)/vmap(transpose(jvp()))/dot_general | solution.py:9
  236.1 29.4 %fusion.35 = f32[1,8192,512]{2,1,0:T(8,128)} fusion(f32[1024,8192]{1,0:T(8,128)} %fusion.51, f32[1024,8192]{1,0:T(8,128)} %fusion.47, bf16[1,1024,512]{2,1,0:T(8,128)(2,1)S(1)} %copy-done.9), kind=kOutput, calls=%fused_computation.45 | convolution fusion | flops 8640266240 | bytes 84934656 | tf_op jit(solution)/vmap(transpose(jvp()))/dot_general | solution.py:9
  266.8 16.2 %convolution_convert_fusion = bf16[1024,8192]{1,0:T(8,128)(2,1)} fusion(bf16[1024,512]{0,1:T(8,128)(2,1)S(1)} %copy-done.13, bf16[2,8192,512]{2,1,0:T(8,128)(2,1)} %param.4), kind=kOutput, calls=%fused_computation.43 | convolution fusion | flops 8598323200 | bytes 26214400 | tf_op jit(solution)/vmap(transpose(jvp()))/dot_general | solution.py:9
  283.0 25.6 %fusion.44 = f32[1,512,8192]{2,1,0:T(8,128)} fusion(bf16[1024,8192]{1,0:T(8,128)(2,1)} %convolution_convert_fusion, f32[1024,8192]{1,0:T(8,128)} %fusion.60, bf16[1,1024,512]{1,2,0:T(8,128)(2,1)S(1)} %copy-done.11, f32[1024]{0:T(1024)S(1)} %copy-done.15), kind=kOutput, calls=%fused_computation.48 | convolution fusion | flops 8641839104 | bytes 68161536 | tf_op jit(solution)/vmap(transpose(jvp()))/dot_general | solution.py:21
  309.8 25.8 %fusion.38 = f32[1,512,8192]{2,1,0:T(8,128)} fusion(bf16[1024,8192]{1,0:T(8,128)(2,1)} %convolution_convert_fusion.1, f32[1024,8192]{1,0:T(8,128)} %fusion.47, bf16[1,1,1024,512]{2,3,1,0:T(8,128)(2,1)S(1)} %copy-done.5, f32[1024]{0:T(1024)S(1)} %bitcast.374), kind=kOutput, calls=%fused_computation.46 | convolution fusion | flops 8641839104 | bytes 68161536 | tf_op jit(solution)/vmap(transpose(jvp()))/dot_general | solution.py:21
  335.7 35.9 %fusion.41 = f32[1,512,8192]{2,1,0:T(8,128)} fusion(f32[1024,8192]{1,0:T(8,128)} %fusion.60, f32[1024,8192]{1,0:T(8,128)} %fusion.58, bf16[1024,8192]{1,0:T(8,128)(2,1)} %convolution_convert_fusion, bf16[1,1024,512]{1,2,0:T(8,128)(2,1)S(1)} %copy-done.11, f32[1024]{0:T(1024)S(1)} %copy-done.15), kind=kOutput, calls=%fused_computation.47 | convolution fusion | flops 8683782144 | bytes 101715968 | tf_op jit(solution)/vmap(transpose(jvp()))/dot_general | solution.py:20
  371.7 15.8 %convolution_bitcast_fusion.1 = f32[1,512,8192]{2,1,0:T(8,128)} fusion(bf16[1024,8192]{1,0:T(8,128)(2,1)} %fusion.6, bf16[1,1,1024,512]{2,3,1,0:T(8,128)(2,1)S(1)} %copy-done.5, f32[1024]{0:T(1024)S(1)} %bitcast.375), kind=kOutput, calls=%fused_computation.50 | convolution fusion | flops 8591507456 | bytes 34607104 | tf_op jit(solution)/vmap(transpose(jvp()))/dot_general | solution.py:20
  391.2 25.0 %reduce-scatter.27.cloned.1.call-done = f32[1,1024,512]{2,1,0:T(8,128)} async-done(((f32[1,8192,512]{2,1,0:T(8,128)}), f32[1,1024,512]{2,1,0:T(8,128)}) %reduce-scatter.27.cloned.1.call-update) | async-done | bytes 2097168
  420.6 85.4 %reduce-scatter.25.cloned.1.call-done = f32[1,64,8192]{2,1,0:T(8,128)} async-done(((f32[1,512,8192]{2,1,0:T(8,128)}), f32[1,64,8192]{2,1,0:T(8,128)}) %reduce-scatter.25.cloned.1.call-update) | async-done | bytes 2097168
  507.7 88.0 %reduce-scatter.23.cloned.1.call-done = f32[1,64,8192]{2,1,0:T(8,128)} async-done(((f32[1,512,8192]{2,1,0:T(8,128)}), f32[1,64,8192]{2,1,0:T(8,128)}) %reduce-scatter.23.cloned.1.call-update) | async-done | bytes 2097168
  600.0 85.9 %reduce-scatter.21.cloned.1.call-done = f32[1,64,8192]{2,1,0:T(8,128)} async-done(((f32[1,512,8192]{2,1,0:T(8,128)}), f32[1,64,8192]{2,1,0:T(8,128)}) %reduce-scatter.21.cloned.1.call-update) | async-done | bytes 2097168
  687.6 88.5 %reduce-scatter.19.cloned.1.call-done = f32[1,64,8192]{2,1,0:T(8,128)} async-done(((f32[1,512,8192]{2,1,0:T(8,128)}), f32[1,64,8192]{2,1,0:T(8,128)}) %reduce-scatter.19.cloned.1.call-update) | async-done | bytes 2097168
  820.1 65.3 %all-gather.14.cloned.1.call-done = bf16[1,2,8192,512]{3,2,1,0:T(8,128)(2,1)} async-done(((bf16[1,2,1024,512]{3,2,1,0:T(8,128)(2,1)}), bf16[1,2,8192,512]{3,2,1,0:T(8,128)(2,1)}) %all-gather.14.cloned.1.call-update) | async-done | bytes 16777232 | tf_op jit(solution)/reshape | solution.py:58
  885.4 83.8 %all-gather.12.cloned.1.call-done = bf16[1,2,512,8192]{3,2,1,0:T(8,128)(2,1)} async-done(((bf16[1,2,64,8192]{3,2,1,0:T(8,128)(2,1)}), bf16[1,2,512,8192]{3,2,1,0:T(8,128)(2,1)}) %all-gather.12.cloned.1.call-update) | async-done | bytes 16777232 | tf_op jit(solution)/reshape | solution.py:58
  969.2 83.8 %all-gather.10.cloned.1.call-done = bf16[1,2,512,8192]{3,2,1,0:T(8,128)(2,1)} async-done(((bf16[1,2,64,8192]{3,2,1,0:T(8,128)(2,1)}), bf16[1,2,512,8192]{3,2,1,0:T(8,128)(2,1)}) %all-gather.10.cloned.1.call-update) | async-done | bytes 16777232 | tf_op jit(solution)/reshape | solution.py:58
  1053.1 16.7 %copy.5 = bf16[2,512,8192]{2,1,0:T(8,128)(2,1)} copy(bf16[2,512,8192]{2,1,0:T(8,128)(2,1)} %bitcast.370) | data formatting | bytes 33554432
  (88 shorter events, 113.3 us)
Async XLA Ops:
  7.2 382.3 %reduce-scatter.29.cloned.1.call-start = ((), (), s32[]{:S(2)}) async-start(), calls=%async_computation.14 | async-start | bytes 18874368
  10.3 64.8 %copy-start.10 = (bf16[1,1024,512]{1,2,0:T(8,128)(2,1)}, bf16[1,1024,512]{1,2,0:T(8,128)(2,1)S(1)}, u32[]{:S(2)}) copy-start(bf16[1,1024,512]{1,2,0:T(8,128)(2,1)S(1)} %copy) | copy-start | bytes 3145732
  10.3 19.4 %copy-start.14 = (f32[1024]{0:T(1024)}, f32[1024]{0:T(1024)S(1)}, u32[]{:S(2)}) copy-start(f32[1024]{0:T(1024)S(1)} %add_rsqrt_fusion) | copy-start | bytes 12292
  10.3 19.4 %copy-start.6 = (bf16[1,1024,512]{2,1,0:T(8,128)(2,1)S(1)}, bf16[1,1024,512]{2,1,0:T(8,128)(2,1)}, u32[]{:S(2)}) copy-start(bf16[1,1024,512]{2,1,0:T(8,128)(2,1)} %param.2) | copy-start | bytes 3145732
  90.0 127.1 %copy-start.4 = (bf16[1,1,1024,512]{2,3,1,0:T(8,128)(2,1)}, bf16[1,1,1024,512]{2,3,1,0:T(8,128)(2,1)S(1)}, u32[]{:S(2)}) copy-start(bf16[1,1,1024,512]{2,3,1,0:T(8,128)(2,1)S(1)} %get-tuple-element.10) | copy-start | bytes 3145732
  90.0 127.0 %copy-start.7 = (f32[1,1,1024]{2,1,0:T(1,128)}, f32[1,1,1024]{2,1,0:T(1,128)S(1)}, u32[]{:S(2)}) copy-start(f32[1,1,1024]{2,1,0:T(1,128)S(1)} %rsqrt.38) | copy-start | bytes 12292
  109.2 18.8 %copy-start.9 = (bf16[1,1024,512]{2,1,0:T(8,128)(2,1)S(1)}, bf16[1,1024,512]{2,1,0:T(8,128)(2,1)}, u32[]{:S(2)}) copy-start(bf16[1,1024,512]{2,1,0:T(8,128)(2,1)} %param.5) | copy-start | bytes 3145732
  236.0 180.2 %reduce-scatter.27.cloned.1.call-start = ((), (), s32[]{:S(2)}) async-start(), calls=%async_computation.13 | async-start | bytes 18874368
  265.6 17.4 %copy-start.11 = (bf16[1,1024,512]{1,2,0:T(8,128)(2,1)S(1)}, bf16[1,1024,512]{1,2,0:T(8,128)(2,1)}, u32[]{:S(2)}) copy-start(bf16[1,1024,512]{1,2,0:T(8,128)(2,1)} %copy-done.10) | copy-start | bytes 3145732
  265.6 17.3 %copy-start.15 = (f32[1024]{0:T(1024)S(1)}, f32[1024]{0:T(1024)}, u32[]{:S(2)}) copy-start(f32[1024]{0:T(1024)} %copy-done.14) | copy-start | bytes 12292
  265.6 240.4 %reduce-scatter.25.cloned.1.call-start = ((), (), s32[]{:S(2)}) async-start(), calls=%async_computation.12 | async-start | bytes 18874368
  308.6 1.2 copy-start.8
  308.6 287.0 %reduce-scatter.23.cloned.1.call-start = ((), (), s32[]{:S(2)}) async-start(), calls=%async_computation.11 | async-start | bytes 18874368
  335.7 350.2 %reduce-scatter.21.cloned.1.call-start = ((), (), s32[]{:S(2)}) async-start(), calls=%async_computation.10 | async-start | bytes 18874368
  371.7 404.4 %reduce-scatter.19.cloned.1.call-start = ((), (), s32[]{:S(2)}) async-start(), calls=%async_computation.9 | async-start | bytes 18874368
  387.6 497.8 %all-gather.14.cloned.1.call-start = ((), (), s32[]{:S(2)}) async-start(), calls=%async_computation.8 | async-start | bytes 18874368 | tf_op jit(solution)/reshape | solution.py:58
  391.2 208.8 %copy-start.2 = (bf16[1,1,1024,512]{3,2,1,0:T(8,128)(2,1)}, bf16[1,1,1024,512]{3,2,1,0:T(8,128)(2,1)S(1)}, u32[]{:S(2)}) copy-start(bf16[1,1,1024,512]{3,2,1,0:T(8,128)(2,1)S(1)} %convert_bitcast_fusion.3) | copy-start | bytes 3145732
  804.3 164.9 %all-gather.12.cloned.1.call-start = ((), (), s32[]{:S(2)}) async-start(), calls=%async_computation.7 | async-start | bytes 18874368 | tf_op jit(solution)/reshape | solution.py:58
  812.3 240.7 %all-gather.10.cloned.1.call-start = ((), (), s32[]{:S(2)}) async-start(), calls=%async_computation.6 | async-start | bytes 18874368 | tf_op jit(solution)/reshape | solution.py:58
  1053.0 16.7 %copy-start = (bf16[1,2,512,8192]{3,2,1,0:T(8,128)(2,1)S(1)}, bf16[1,2,512,8192]{3,2,1,0:T(8,128)(2,1)}, u32[]{:S(2)}) copy-start(bf16[1,2,512,8192]{3,2,1,0:T(8,128)(2,1)} %all-gather.12.cloned.1.call-done) | copy-start | bytes 50331652
  1053.0 25.2 %slice-start = ((s8[16777216]{0:T(1024)(128)(4,1)}), s8[4194304]{0:T(1024)(128)(4,1)S(1)}, s32[]{:S(2)}) async-start(s8[16777216]{0:T(1024)(128)(4,1)} %bitcast.366), calls=%async_computation.15 | async-start | bytes 8388608
  1053.1 25.2 %slice-start.1 = ((s8[16777216]{0:T(1024)(128)(4,1)}), s8[4194304]{0:T(1024)(128)(4,1)S(1)}, s32[]{:S(2)}) async-start(s8[16777216]{0:T(1024)(128)(4,1)} %bitcast.366), calls=%async_computation.16 | async-start | bytes 8388608
  1069.7 10.0 slice-start.2
  1069.7 11.2 %slice-start.3 = ((s8[16777216]{0:T(1024)(128)(4,1)}), s8[4194304]{0:T(1024)(128)(4,1)S(1)}, s32[]{:S(2)}) async-start(s8[16777216]{0:T(1024)(128)(4,1)} %bitcast.366), calls=%async_computation.18 | async-start | bytes 8388608
  (6 other events, 6.0 us)
Sparse Core Ops, SparseCore 0:
  236.2 90.1 reduce-scatter.28
  328.7 87.3 reduce-scatter.26
  418.5 87.3 reduce-scatter.24
  508.2 87.3 reduce-scatter.22
  598.4 87.3 reduce-scatter.20
  688.6 87.3 reduce-scatter.18
  804.4 80.9 all-gather.13
  887.6 81.6 all-gather.11
  971.4 81.6 all-gather.9
where the time goes:
time: 1100 us; the launch traced here: 1090 us
  waiting for transfers between devices  606 us (55%)
  matrix products  310 us (28%)
  other arithmetic  103 us (9%)
  local copies, waits for them, and re-layouts  42 us (4%)
  between operations  17.9 us (2%)
  blocking collectives  14 us (1%)
    unnamed x15, waiting for transfers between devices  373 us
    reshape x3, waiting for transfers between devices, step(): t.reshape(-1, *t.shape[2:])  233 us
    dot_general x5, matrix products, layer(): up = jnp.dot(a, w['w_up'], preferred_element_type=jnp.float32)  112 us
    dot_general x5, matrix products, layer(): gate = jnp.dot(a, w['w_gate'], preferred_element_type=jnp.float32)  106 us
    dot_general x5, matrix products, matmul(): jnp.dot(a, w, preferred_element_type=jnp.float32).astype(jnp.bfloat16)  91.8 us
    unnamed x4, other arithmetic  62.7 us
    unnamed x47, local copies, waits for them, and re-layouts  41.4 us
    reshape x3, other arithmetic, step(): t.reshape(-1, *t.shape[2:])  23.7 us
  transfers between devices with their start and end apart: 9, of which 8 were waited for; matrix products, arithmetic and copies ran while one was open for 16% of the time, Pallas kernels for 0%

commit v1 on v0

v1 whole, which is shorter than its diff:
```python
import functools

import jax
import jax.numpy as jnp
from jax import lax
from jax.experimental import pallas as pl
from jax.experimental.pallas import tpu as pltpu
from jax.sharding import PartitionSpec as P

BF16, F32 = jnp.bfloat16, jnp.float32
MESH = pl.DeviceIdType.MESH
LANES = 128
TILE = 256
ROWS = 256
SLOTS = 4
LAG2, LAG3 = 2, 3


def dot(a, b):
    return jnp.dot(a, b, preferred_element_type=F32)


def dot_t(a, b):
    return lax.dot_general(a, b, (((1,), (1,)), ((), ())), preferred_element_type=F32)


def sigmoid(x):
    return 0.5 * jnp.tanh(0.5 * x) + 0.5


def step_kernel(
    n, x_hbm, dy_hbm, wg_hbm, wu_hbm, wd_hbm, gg_hbm, gu_hbm, gd_hbm, factor_ref,
    x_v, dy_v, h_v, a_v, at_v, ct_v, ctt_v, acc, wg, wu, wd, gs, us, ds, own, drecv, h1, h2, gg, gu, gd, ss, ss_all,
    in_sem, w_sem, out_sem, d_send, d_recv, h1_send, h1_recv, h2_send, h2_recv, cr_p, cr_n, ss_send, ss_recv,
):
    layers, width, units = wg_hbm.shape
    share = width // n
    per = units // n
    chunks = per // LANES
    chunk = n * LANES
    total = layers * chunks
    block = own.shape[3]
    half = block // 2
    chips = n // 2
    tiles = chunk // TILE

    me = lax.axis_index("dp")
    c, k = lax.div(me, 2), lax.rem(me, 2)
    c_right, c_left, c_far = lax.rem(c + 1, chips), lax.rem(c + chips - 1, chips), lax.rem(c + 2, chips)
    right, left, other = c_right * 2 + k, c_left * 2 + k, c * 2 + (1 - k)

    barrier = pltpu.get_barrier_semaphore()
    for away in range(1, n):
        pl.semaphore_signal(barrier, inc=1, device_id={"dp": lax.rem(me + away, n)}, device_id_type=MESH)

    def fetch(t):
        slot, number, j = lax.rem(t, 2), lax.rem(lax.div(t, chunks), layers), lax.rem(t, chunks)
        for i in range(n):
            at = pl.ds(pl.multiple_of(i * per + j * LANES, LANES), LANES)
            here = pl.ds(i * LANES, LANES)
            pltpu.make_async_copy(wg_hbm.at[number, :, at], wg.at[slot, :, here], w_sem.at[0, slot]).start()
            pltpu.make_async_copy(wu_hbm.at[number, :, at], wu.at[slot, :, here], w_sem.at[1, slot]).start()
            pltpu.make_async_copy(wd_hbm.at[number, at, :], wd.at[slot, here, :], w_sem.at[2, slot]).start()

    def fetched(t):
        slot = lax.rem(t, 2)
        pltpu.make_async_copy(wg.at[slot], wg.at[slot], w_sem.at[0, slot]).wait()
        pltpu.make_async_copy(wu.at[slot], wu.at[slot], w_sem.at[1, slot]).wait()
        pltpu.make_async_copy(wd.at[slot], wd.at[slot], w_sem.at[2, slot]).wait()

    load_x = pltpu.make_async_copy(x_hbm.at[0], x_v, in_sem.at[0])
    load_dy = pltpu.make_async_copy(dy_hbm.at[0], dy_v, in_sem.at[1])
    load_x.start()
    fetch(0)
    load_dy.start()
    load_x.wait()

    tokens = x_v.shape[0]
    blocks = [slice(r, r + ROWS) for r in range(0, tokens, ROWS)]

    def scale_of(wide):
        return lax.rsqrt(jnp.mean(wide * wide, -1, keepdims=True) + 1e-6)

    def normed(src, rows):
        wide = src[rows, :].astype(F32)
        a = (wide * scale_of(wide)).astype(BF16)
        a_v[rows, :] = a
        at_v[:, rows] = a.T

    for rows in blocks:
        normed(x_v, rows)
    acc[...] = jnp.zeros_like(acc)

    def forward(t, _):
        slot = lax.rem(t, 2)
        fetched(t)
        fetch(t + 1)
        for f in range(tiles):
            cols = slice(f * TILE, (f + 1) * TILE)
            gate = dot(a_v[...], wg[slot, :, cols])
            up = dot(a_v[...], wu[slot, :, cols])
            act = (gate * sigmoid(gate) * up).astype(BF16)
            acc[...] += dot(act, wd[slot, cols, :])
        return 0

    lax.fori_loop(0, chunks, forward, 0)
    load_dy.wait()
    for rows in blocks:
        h_v[rows, :] = (x_v[rows, :].astype(F32) + acc[rows, :].astype(BF16).astype(F32)).astype(BF16)
        normed(h_v, rows)
        ct_v[rows, :] = dy_v[rows, :]
        ctt_v[:, rows] = dy_v[rows, :].T
    acc[...] = jnp.zeros_like(acc)
    ss[...] = jnp.zeros_like(ss)
    pl.semaphore_wait(barrier, n - 1)

    def to(src, dst, send, recv, device):
        return pltpu.make_async_remote_copy(src, dst, send, recv, device_id={"dp": device}, device_id_type=MESH)

    def across(s):
        slot = lax.rem(s, SLOTS)
        return to(own.at[slot, 1 - k], drecv.at[slot], d_send.at[slot], d_recv.at[slot], other)

    def hop1(s, way):
        slot = lax.rem(s, SLOTS)
        rows = pl.ds(half, half) if way == 0 else pl.ds(0, half)
        return to(own.at[slot, k, c_far, rows], h1.at[slot, way], h1_send.at[slot, way], h1_recv.at[slot, way], (right, left)[way])

    def hop2(s, way):
        slot = lax.rem(s, SLOTS)
        return to(own.at[slot, k, (c_right, c_left)[way]], h2.at[slot, way], h2_send.at[slot, way], h2_recv.at[slot, way], (right, left)[way])

    def wide(ref):
        return ref[...].astype(F32)

    def t0(s):
        @pl.when(s >= SLOTS)
        def _():
            pl.semaphore_wait(cr_p, 1)

        across(s).start()

    def t1(s):
        slot = lax.rem(s, SLOTS)
        across(s).wait_recv()
        mine = own.at[slot, k, c_far]
        mine[...] = (wide(mine) + wide(drecv.at[slot, c_far])).astype(BF16)

        @pl.when(s >= SLOTS)
        def _():
            for way in range(2):
                pl.semaphore_wait(cr_n.at[way], 1)

        for way in range(2):
            hop1(s, way).start()

    def t2(s):
        slot = lax.rem(s, SLOTS)
        for way in range(2):
            hop1(s, way).wait_recv()
        for way in range(2):
            chip = (c_right, c_left)[way]
            for part in range(2):
                rows = pl.ds(part * half, half)
                mine = own.at[slot, k, chip, rows]
                value = wide(mine) + wide(drecv.at[slot, chip, rows])
                if part == 1 - way:
                    value += wide(h1.at[slot, way])
                mine[...] = value.astype(BF16)
        for way in range(2):
            hop2(s, way).start()

    def t3(s):
        slot = lax.rem(s, SLOTS)
        number, j = layers - 1 - lax.div(s, chunks), lax.rem(s, chunks)
        for way in range(2):
            hop2(s, way).wait_recv()
        lane = pl.ds(pl.multiple_of(j * LANES, LANES), LANES)

        def summed(start, size):
            rows = pl.ds(start, size)
            value = wide(own.at[slot, k, c, rows]) + wide(drecv.at[slot, c, rows])
            value = (value + wide(h2.at[slot, 0, rows]) + wide(h2.at[slot, 1, rows])).astype(BF16)
            return value, jnp.sum((value.astype(F32) ** 2).reshape(size // 8, 8, LANES), 0)

        value, squares = summed(0, width)
        gd[number, lane, :] = value.astype(F32).T.astype(BF16)
        for base, g in ((width, gg), (width + n * share, gu)):
            for i in range(n):
                value, more = summed(base + i * share, share)
                g[number, :, pl.ds(pl.multiple_of(i * per + j * LANES, LANES), LANES)] = value
                squares += more
        ss[...] += squares
        across(s).wait_send()
        for way in range(2):
            hop1(s, way).wait_send()
            hop2(s, way).wait_send()

        @pl.when(s + SLOTS < total)
        def _():
            pl.semaphore_signal(cr_p, inc=1, device_id={"dp": other}, device_id_type=MESH)
            pl.semaphore_signal(cr_n.at[0], inc=1, device_id={"dp": left}, device_id_type=MESH)
            pl.semaphore_signal(cr_n.at[1], inc=1, device_id={"dp": right}, device_id_type=MESH)

        @pl.when(j == chunks - 1)
        def _():
            for i, (src, dst) in enumerate(((gg, gg_hbm), (gu, gu_hbm), (gd, gd_hbm))):
                pltpu.make_async_copy(src.at[number], dst.at[number], out_sem.at[i, number]).start()

    def ticks(s):
        @pl.when(jnp.logical_and(s >= 2, s <= total))
        def _():
            t1(s - 1)

        @pl.when(jnp.logical_and(s >= LAG2, s < total + LAG2))
        def _():
            t2(s - LAG2)

        @pl.when(s >= LAG3)
        def _():
            t3(s - LAG3)

    def store(slot, f, base, value):
        value = value.astype(BF16)
        for i in range(TILE // LANES):
            at = f * (TILE // LANES) + i
            part = value[:, i * LANES : (i + 1) * LANES]
            if base == 0:
                own[slot, at % 2, at // 2, 0:width, :] = part
            else:
                first = base + at * share
                for o in range(n):
                    own[slot, o % 2, o // 2, first : first + share, :] = part[o * share : (o + 1) * share, :]

    def backward(last, first, s, _):
        t = s + chunks
        slot, keep = lax.rem(t, 2), lax.rem(s, SLOTS)
        fetched(t)
        if first:

            @pl.when(s < total - 1)
            def _():
                fetch(t + 1)

        else:
            fetch(t + 1)
        for f in range(tiles):
            cols = slice(f * TILE, (f + 1) * TILE)
            gs[...] = dot(a_v[...], wg[slot, :, cols])
            us[...] = dot(a_v[...], wu[slot, :, cols])
            ds[...] = dot_t(ct_v[...], wd[slot, cols, :]).astype(BF16)
            gate, up, dact = gs[...], us[...], wide(ds)
            sig = sigmoid(gate)
            silu = gate * sig
            act = (silu * up).astype(BF16)
            dup = (dact * silu).astype(BF16)
            dgate = (dact * up * (sig + silu * (1 - sig))).astype(BF16)
            store(keep, f, 0, dot(ctt_v[...], act))
            store(keep, f, width, dot(at_v[...], dgate))
            store(keep, f, width + n * share, dot(at_v[...], dup))
            if not first:
                acc[...] += dot_t(dgate, wg[slot, :, cols]) + dot_t(dup, wu[slot, :, cols])
            if f == 0:
                ticks(s)
        t0(s)
        if last:

            @pl.when(s == 0)
            def _():
                t1(s)

        return 0

    lax.fori_loop(0, chunks, functools.partial(backward, True, False), 0)
    for rows in blocks:
        u = acc[rows, :].astype(BF16).astype(F32)
        h = h_v[rows, :].astype(F32)
        scale = scale_of(h)
        dh = scale * u - h * (scale * scale * scale * jnp.mean(u * h, -1, keepdims=True))
        ct = (dy_v[rows, :].astype(F32) + dh.astype(BF16).astype(F32)).astype(BF16)
        ct_v[rows, :] = ct
        ctt_v[:, rows] = ct.T
        normed(x_v, rows)
    lax.fori_loop(chunks, total, functools.partial(backward, False, True), 0)

    def drain(s, _):
        ticks(s)
        return 0

    lax.fori_loop(total, total + LAG3, drain, 0)

    def squares_to(away):
        peer = lax.rem(me + away, n)
        return to(ss, ss_all.at[me], ss_send.at[away], ss_recv.at[me], peer)

    for away in range(1, n):
        squares_to(away).start()
    ss_all[me] = ss[...]
    for away in range(1, n):
        peer = lax.rem(me + away, n)
        to(ss, ss_all.at[peer], ss_send.at[away], ss_recv.at[peer], peer).wait_recv()
    everyone = ss_all[0]
    for i in range(1, n):
        everyone += ss_all[i]
    mean = jnp.sum(jnp.sum(everyone, 1, keepdims=True), 0, keepdims=True) / (3.0 * layers * width * units)
    factor_ref[...] = jnp.broadcast_to(jnp.minimum(1.0, 0.5 * lax.rsqrt(mean + 1e-30)), factor_ref.shape)
    for away in range(1, n):
        squares_to(away).wait_send()
    for i, (src, dst) in enumerate(((gg, gg_hbm), (gu, gu_hbm), (gd, gd_hbm))):
        for number in range(layers):
            pltpu.make_async_copy(src.at[number], dst.at[number], out_sem.at[i, number]).wait()


def gradients(n, x, dy, w_gate, w_up, w_down):
    layers, width, units = w_gate.shape
    tokens = x.shape[1]
    share, per, chunk = width // n, units // n, n * LANES
    block = width + 2 * n * share
    hbm, vmem = pl.BlockSpec(memory_space=pl.ANY), pl.BlockSpec(memory_space=pltpu.VMEM)
    dma, regular = pltpu.SemaphoreType.DMA, pltpu.SemaphoreType.REGULAR
    return pl.pallas_call(
        functools.partial(step_kernel, n),
        out_shape=[
            jax.ShapeDtypeStruct((layers, share, units), BF16),
            jax.ShapeDtypeStruct((layers, share, units), BF16),
            jax.ShapeDtypeStruct((layers, per, width), BF16),
            jax.ShapeDtypeStruct((8, LANES), F32),
        ],
        in_specs=[hbm] * 5,
        out_specs=[hbm] * 3 + [vmem],
        scratch_shapes=[
            *[pltpu.VMEM((tokens, width), BF16)] * 4,
            pltpu.VMEM((width, tokens), BF16),
            pltpu.VMEM((tokens, width), BF16),
            pltpu.VMEM((width, tokens), BF16),
            pltpu.VMEM((tokens, width), F32),
            pltpu.VMEM((2, width, chunk), BF16),
            pltpu.VMEM((2, width, chunk), BF16),
            pltpu.VMEM((2, chunk, width), BF16),
            pltpu.VMEM((tokens, TILE), F32),
            pltpu.VMEM((tokens, TILE), F32),
            pltpu.VMEM((tokens, TILE), BF16),
            pltpu.VMEM((SLOTS, 2, n // 2, block, LANES), BF16),
            pltpu.VMEM((SLOTS, n // 2, block, LANES), BF16),
            pltpu.VMEM((SLOTS, 2, block // 2, LANES), BF16),
            pltpu.VMEM((SLOTS, 2, block, LANES), BF16),
            pltpu.VMEM((layers, share, units), BF16),
            pltpu.VMEM((layers, share, units), BF16),
            pltpu.VMEM((layers, per, width), BF16),
            pltpu.VMEM((8, LANES), F32),
            pltpu.VMEM((n, 8, LANES), F32),
            dma((2,)),
            dma((3, 2)),
            dma((3, layers)),
            dma((SLOTS,)),
            dma((SLOTS,)),
            dma((SLOTS, 2)),
            dma((SLOTS, 2)),
            dma((SLOTS, 2)),
            dma((SLOTS, 2)),
            regular,
            regular((2,)),
            dma((n,)),
            dma((n,)),
        ],
        compiler_params=pltpu.CompilerParams(collective_id=0, has_side_effects=True, vmem_limit_bytes=63 * 1024 * 1024),
        name="step",
    )(x, dy, w_gate, w_up, w_down)


def adamw(w, m, v, g):
    m = 0.9 * m + 0.1 * g
    v = 0.95 * v + 0.05 * g * g
    step = m * lax.rsqrt(v + 1e-8) + 0.1 * w
    return (w - 0.02 * step).astype(BF16), m, v


def solution(mesh):
    n = mesh.shape["dp"]

    def on_a_device(x, dy, *arrays):
        weights, ms, vs = (arrays[i : i + 3] for i in (0, 3, 6))
        *grads, factor = gradients(n, x, dy, *weights)
        factor = factor[0, 0]
        me = lax.axis_index("dp")
        new = []
        for w, m, v, g in zip(weights, ms, vs, grads, strict=True):
            rows = w.shape[1] // n
            mine = lax.dynamic_slice_in_dim(w, me * rows, rows, 1)
            w, m, v = adamw(mine.astype(F32), m, v, g.astype(F32) * factor)
            new.append((lax.all_gather(w, "dp", axis=1, tiled=True), m, v))
        return tuple(one[which] for which in range(3) for one in new)

    one, every, block = P(("rep", "dp"), None, None), P(None, None, None), P(None, "dp", None)
    return jax.shard_map(
        on_a_device,
        mesh=mesh,
        in_specs=(one, one, *[every] * 3, *[block] * 6),
        out_specs=(*[P("rep", None, None)] * 3, *[P("rep", "dp", None)] * 6),
        check_vma=False,
    )
```

time: 1100 us -> 576 us (0.52)
  waiting for transfers between devices: 606 us -> 233 us
  matrix products: 310 us -> 0 us
  Pallas kernels: 0 us -> 268 us
  other arithmetic: 103 us -> 25.6 us
  blocking collectives: 14 us -> 0 us
    unnamed x15 -> x3, waiting for transfers between devices: 373 us -> 0.16 us
    dot_general x15 -> x0, matrix products: 310 us -> none  [the longest x5 112 us: layer(): up = jnp.dot(a, w['w_up'], preferred_element_type=jnp.float32)]
    pallas_call x0 -> x1, Pallas kernels: none -> 268 us  [gradients(): pl.pallas_call(functools.partial(step_kernel, n), out_shape=[jax.ShapeDty...]
    reshape x3 -> x0, waiting for transfers between devices: 233 us -> none  [step(): t.reshape(-1, *t.shape[2:])]
    all_gather x0 -> x3, waiting for transfers between devices: none -> 233 us  [on_a_device(): new.append((lax.all_gather(w, 'dp', axis=1, tiled=True), m, v))]
    unnamed x4 -> x1, other arithmetic: 62.7 us -> 0.01 us
    convert_element_type x0 -> x3, other arithmetic: none -> 25.6 us  [adamw(): return ((w - 0.02 * step).astype(BF16), m, v)]
    reshape x3 -> x0, other arithmetic: 23.7 us -> none  [step(): t.reshape(-1, *t.shape[2:])]
  transfers between devices with their start and end apart: 9 -> 3, of which waited for: 8 -> 3; matrix products, arithmetic and copies ran while one was open for 16% -> 3% of each run, Pallas kernels for 0% -> 0%
where the time goes in v1:
time: 576 us
  Pallas kernels  268 us (47%)
  waiting for transfers between devices  233 us (40%)
  local copies, waits for them, and re-layouts  35.3 us (6%)
  other arithmetic  25.6 us (4%)
  between operations  13.8 us (2%)
    pallas_call x1, Pallas kernels, gradients(): pl.pallas_call(functools.partial(step_kernel, n), out_shape=[jax.ShapeDty...  268 us
    all_gather x3, waiting for transfers between devices, on_a_device(): new.append((lax.all_gather(w, 'dp', axis=1, tiled=True), m, v))  233 us
    unnamed x15, local copies, waits for them, and re-layouts  34.1 us
    convert_element_type x3, other arithmetic, adamw(): return ((w - 0.02 * step).astype(BF16), m, v)  25.6 us
  transfers between devices with their start and end apart: 3, of which 3 were waited for; matrix products, arithmetic and copies ran while one was open for 3% of the time, Pallas kernels for 0%

profile of v1, /device:TPU:113, one launch (start us, length us, event | category | flops | bytes accessed | tf_op | source)
XLA Modules:
  0.0 575.6 jit_solution(4814501310001856172)
XLA Ops:
  7.2 0.1 all-gather.4.cloned.1.call-start
  7.3 267.7 %step.1 = (bf16[2,64,8192]{2,1,0:T(8,128)(2,1)}, bf16[2,64,8192]{2,1,0:T(8,128)(2,1)}, bf16[2,1024,512]{2,1,0:T(8,128)(2,1)}, f32[8,128]{1,0:T(8,128)}) custom-call(bf16[1,1024,512]{2,1,0:T(8,128)(2,1)} %x_hbm.1, bf16[1,1024,512]{2,1,0:T(8,128)(2,1)} %dy_hbm.1, bf16[2,512,8192]{2,1,0:T(8,128)(2,1)} %wg_hbm.1, bf16[2,512,8192]{2,1,0:T(8,128)(2,1)} %wu_hbm.1, ...), custom_call_target="tpu_custom_call" | custom-call | tf_op jit(solution)/shard_map/step/pallas_call | solution.py:321
  275.0 1.2 slice.3
  276.2 8.9 %fusion.2 = (bf16[2,64,8192]{2,1,0:T(8,128)(2,1)}, f32[2,64,8192]{2,1,0:T(8,128)}, f32[2,64,8192]{2,1,0:T(8,128)}) fusion(bf16[2,512,8192]{2,1,0:T(8,128)(2,1)} %wg_hbm.1, s32[]{:T(128)S(6)} %select_n.7, f32[]{:T(128)} %bitcast, bf16[2,64,8192]{2,1,0:T(8,128)(2,1)} %get-tuple-element.13, f32[2,64,8192]{2,1,0:T(8,128)} %param.19, f32[2,64,8192]{2,1,0:T(8,128)} %param.16), kind=kLoop, calls=%fused_computation.11 | loop fusion | flops 17825792 | bytes 23068680 | tf_op jit(solution)/shard_map/convert_element_type | solution.py:375
  285.1 0.1 all-gather.4.cloned.1.call-update
  285.2 0.1 all-gather.8.cloned.1.call-start
  285.3 0.0 copy-start.1
  285.3 9.0 %fusion.8 = (bf16[2,1024,512]{2,1,0:T(8,128)(2,1)}, f32[2,1024,512]{2,1,0:T(8,128)}, f32[2,1024,512]{2,1,0:T(8,128)}) fusion(bf16[2,8192,512]{2,1,0:T(8,128)(2,1)} %wd_hbm.1, s32[]{:T(128)S(6)} %select_n.8, f32[]{:T(128)} %bitcast, bf16[2,1024,512]{2,1,0:T(8,128)(2,1)} %get-tuple-element.16, f32[2,1024,512]{2,1,0:T(8,128)} %param.21, f32[2,1024,512]{2,1,0:T(8,128)} %param.18), kind=kLoop, calls=%fused_computation.17 | loop fusion | flops 17825792 | bytes 23068680 | tf_op jit(solution)/shard_map/convert_element_type | solution.py:375
  294.3 0.1 all-gather.8.cloned.1.call-update
  294.4 0.1 all-gather.6.cloned.1.call-start
  294.4 0.0 copy-done.1
  294.5 7.7 %fusion.5 = (bf16[2,64,8192]{2,1,0:T(8,128)(2,1)}, f32[2,64,8192]{2,1,0:T(8,128)}, f32[2,64,8192]{2,1,0:T(8,128)}) fusion(bf16[2,512,8192]{2,1,0:T(8,128)(2,1)} %wu_hbm.1, s32[]{:T(128)S(6)} %select_n.7, f32[]{:T(128)} %bitcast, bf16[2,64,8192]{2,1,0:T(8,128)(2,1)S(1)} %copy-done.1, f32[2,64,8192]{2,1,0:T(8,128)} %param.20, f32[2,64,8192]{2,1,0:T(8,128)} %param.17), kind=kLoop, calls=%fused_computation.14 | loop fusion | flops 17825792 | bytes 23068680 | tf_op jit(solution)/shard_map/convert_element_type | solution.py:375
  302.1 0.1 all-gather.6.cloned.1.call-update
  302.2 65.2 %all-gather.4.cloned.1.call-done = bf16[2,512,8192]{2,1,0:T(8,128)(2,1)} async-done(((bf16[2,64,8192]{2,1,0:T(8,128)(2,1)}), bf16[2,512,8192]{2,1,0:T(8,128)(2,1)}) %all-gather.4.cloned.1.call-update) | async-done | bytes 16777232 | tf_op jit(solution)/shard_map/all_gather | solution.py:391
  367.4 83.8 %all-gather.8.cloned.1.call-done = bf16[2,8192,512]{2,1,0:T(8,128)(2,1)} async-done(((bf16[2,1024,512]{2,1,0:T(8,128)(2,1)}), bf16[2,8192,512]{2,1,0:T(8,128)(2,1)}) %all-gather.8.cloned.1.call-update) | async-done | bytes 16777232 | tf_op jit(solution)/shard_map/all_gather | solution.py:391
  451.2 83.8 %all-gather.6.cloned.1.call-done = bf16[2,512,8192]{2,1,0:T(8,128)(2,1)} async-done(((bf16[2,64,8192]{2,1,0:T(8,128)(2,1)}), bf16[2,512,8192]{2,1,0:T(8,128)(2,1)}) %all-gather.6.cloned.1.call-update) | async-done | bytes 16777232 | tf_op jit(solution)/shard_map/all_gather | solution.py:391
  535.0 16.7 %copy.23 = bf16[2,512,8192]{2,1,0:T(8,128)(2,1)} copy(bf16[2,512,8192]{2,1,0:T(8,128)(2,1)} %all-gather.4.cloned.1.call-done) | data formatting | bytes 33554432
  551.7 0.0 copy-done
  551.7 8.5 %copy.24 = bf16[2,512,8192]{2,1,0:T(8,128)(2,1)} copy(bf16[2,512,8192]{2,1,0:T(8,128)(2,1)S(1)} %copy-done) | data formatting | bytes 33554432
  560.2 0.0 slice-done
  560.2 0.0 slice-done.1
  560.2 1.5 slice-done.2
  561.7 1.2 slice-done.3
  562.9 6.2 %copy.25 = bf16[2,8192,512]{2,1,0:T(8,128)(2,1)} copy(bf16[2,8192,512]{2,1,0:T(8,128)(2,1)S(1)} %bitcast.2) | data formatting | bytes 33554432
  (6 shorter events, 0.0 us)
Async XLA Ops:
  7.2 360.2 %all-gather.4.cloned.1.call-start = ((), (), s32[]{:S(2)}) async-start(), calls=%async_computation | async-start | bytes 18874368 | tf_op jit(solution)/shard_map/all_gather | solution.py:391
  285.2 166.0 %all-gather.8.cloned.1.call-start = ((), (), s32[]{:S(2)}) async-start(), calls=%async_computation.2 | async-start | bytes 18874368 | tf_op jit(solution)/shard_map/all_gather | solution.py:391
  285.3 9.2 %copy-start.1 = (bf16[2,64,8192]{2,1,0:T(8,128)(2,1)S(1)}, bf16[2,64,8192]{2,1,0:T(8,128)(2,1)}, u32[]{:S(2)}) copy-start(bf16[2,64,8192]{2,1,0:T(8,128)(2,1)} %get-tuple-element.15) | copy-start | bytes 6291460
  294.4 240.7 %all-gather.6.cloned.1.call-start = ((), (), s32[]{:S(2)}) async-start(), calls=%async_computation.1 | async-start | bytes 18874368 | tf_op jit(solution)/shard_map/all_gather | solution.py:391
  535.0 16.7 %copy-start = (bf16[2,512,8192]{2,1,0:T(8,128)(2,1)S(1)}, bf16[2,512,8192]{2,1,0:T(8,128)(2,1)}, u32[]{:S(2)}) copy-start(bf16[2,512,8192]{2,1,0:T(8,128)(2,1)} %all-gather.6.cloned.1.call-done) | copy-start | bytes 50331652
  535.0 25.2 %slice-start = ((s8[16777216]{0:T(1024)(128)(4,1)}), s8[4194304]{0:T(1024)(128)(4,1)S(1)}, s32[]{:S(2)}) async-start(s8[16777216]{0:T(1024)(128)(4,1)} %bitcast.1), calls=%async_computation.3 | async-start | bytes 8388608
  535.0 25.2 %slice-start.1 = ((s8[16777216]{0:T(1024)(128)(4,1)}), s8[4194304]{0:T(1024)(128)(4,1)S(1)}, s32[]{:S(2)}) async-start(s8[16777216]{0:T(1024)(128)(4,1)} %bitcast.1), calls=%async_computation.4 | async-start | bytes 8388608
  551.7 10.0 %slice-start.2 = ((s8[16777216]{0:T(1024)(128)(4,1)}), s8[4194304]{0:T(1024)(128)(4,1)S(1)}, s32[]{:S(2)}) async-start(s8[16777216]{0:T(1024)(128)(4,1)} %bitcast.1), calls=%async_computation.5 | async-start | bytes 8388608
  551.7 11.2 %slice-start.3 = ((s8[16777216]{0:T(1024)(128)(4,1)}), s8[4194304]{0:T(1024)(128)(4,1)S(1)}, s32[]{:S(2)}) async-start(s8[16777216]{0:T(1024)(128)(4,1)} %bitcast.1), calls=%async_computation.6 | async-start | bytes 8388608
Sparse Core Ops, SparseCore 0:
  285.3 82.0 all-gather.3
  369.6 81.6 all-gather.7
  453.4 81.6 all-gather.5
